TPU v7x, 32 devices: a whole 2x2x4 slice. The times are simulated.
32 devices in a mesh: dp: 4 (over z), tensor: 8 (over y, x, core).
Axes of the slice: x: 2, y: 2, z: 4, core: 2. Of those that a mesh axis runs over, the one named last changes fastest.
Arguments:
- gradient: bfloat16 [4, 2560, 8192], P('dp', None, 'tensor'), may hold values from -6 to 6
- feedback: float32 [4, 2560, 8192], P('dp', None, 'tensor'), may hold values from -4 to 4
- q_start: float32 [8192, 32], P('tensor'), may hold values from -6 to 6
Outputs:
- p_factor: float32 [2560, 32], P('tensor')
- q_factor: float32 [8192, 32], P('tensor')
- decoded: float32 [2560, 8192], P(None, 'tensor')
- residual: float32 [4, 2560, 8192], P('dp', None, 'tensor')
All inputs are finite; a program needn't handle non-finite values.
Results may differ from a plain program's by a relative error of at most 0.0003.
Values sent between devices are 32-bit elements; how exact they have to be, the bound alone decides.
A program may use at most 64 MiB of HBM per device.

v0:
```python
import jax
import jax.numpy as jnp
from jax import lax
from jax.sharding import PartitionSpec as P


def orthonormal(p_sum, gram_matrix):
    factor_low = jnp.linalg.cholesky(gram_matrix)
    return jax.scipy.linalg.solve_triangular(factor_low, p_sum.T, lower=True).T


def local(gradient, feedback, q_start):
    high = lax.Precision.HIGHEST
    merged = gradient[0].astype(jnp.float32) + feedback[0]
    row_block = lax.psum_scatter(
        jnp.dot(merged, q_start, precision=high), "tensor", scatter_dimension=0, tiled=True
    )
    row_block = lax.psum(row_block, "dp")
    gram_matrix = lax.psum(jnp.dot(row_block.T, row_block, precision=high), "tensor")
    p_factor = orthonormal(row_block, gram_matrix)
    basis_all = lax.all_gather(p_factor, "tensor", axis=0, tiled=True)
    q_local = lax.dot_general(merged, basis_all, (((0,), (0,)), ((), ())), precision=high)
    q_factor = lax.psum(q_local, "dp") / lax.axis_size("dp")
    decoded = jnp.dot(basis_all, q_factor.T, precision=high)
    residual = merged - decoded
    return (p_factor, q_factor, decoded, residual[None])


def solution(mesh):
    in_specs = (P("dp", None, "tensor"), P("dp", None, "tensor"), P("tensor", None))
    out_specs = (P("tensor", None), P("tensor", None), P(None, "tensor"), P("dp", None, "tensor"))
    return jax.shard_map(local, mesh=mesh, in_specs=in_specs, out_specs=out_specs, check_vma=False)
```

profile of v0, /device:TPU:0, one launch (start us, length us, event | category | flops | bytes accessed | tf_op | source)
XLA Modules:
  0.0 192.3 jit_solution(12324662725646355803)
XLA Ops:
  7.2 0.0 copy-start
  7.2 0.0 reduce-scatter.4.cloned.1.call-start
  7.2 0.8 copy-done
  8.1 12.6 %fusion.2 = f32[2560,32]{1,0:T(8,128)} fusion(f32[1024,32]{0,1:T(8,128)S(1)} %copy-done, f32[1,2560,1024]{2,1,0:T(8,128)} %param.4, bf16[1,2560,1024]{2,1,0:T(8,128)(2,1)} %param.3), kind=kOutput, calls=%fused_computation.3 | convolution fusion | flops 1011875840 | bytes 16187392
  20.7 0.0 reduce-scatter.4.cloned.1.call-update
  20.7 0.0 all-reduce.2.cloned.1.call-start
  20.8 40.0 %reduce-scatter.4.cloned.1.call-done = f32[320,32]{1,0:T(8,128)} async-done(((f32[2560,32]{1,0:T(8,128)}), f32[320,32]{1,0:T(8,128)}) %reduce-scatter.4.cloned.1.call-update) | async-done | bytes 40976
  60.8 1.0 copy.17
  61.8 19.5 %psum.21 = f32[320,32]{0,1:T(8,128)S(1)} all-reduce(f32[320,32]{0,1:T(8,128)S(1)} %copy.17), channel_id=1, replica_groups=mesh['dp'=4,'tensor'=8] {'dp'}, use_global_device_ids=true, to_apply=%region_1.0 | all-reduce | flops 10240 | bytes 81920 | tf_op jit(solution)/shard_map/psum | solution.py:18
  81.3 0.2 fusion.9
  81.5 22.3 %psum.22 = f32[32,32]{0,1:T(8,128)S(1)} all-reduce(f32[32,32]{0,1:T(8,128)S(1)} %fusion.9), channel_id=1, replica_groups=mesh['dp'=4,'tensor'=8] {'tensor'}, use_global_device_ids=true, to_apply=%region_2.0 | all-reduce | flops 1024 | bytes 8192 | tf_op jit(solution)/shard_map/psum | solution.py:19
  103.8 0.1 copy.13
  103.9 2.9 %cholesky.16 = f32[32,32]{1,0:T(8,128)S(1)} custom-call(f32[32,32]{1,0:T(8,128)S(1)} %fusion.8), custom_call_target="Cholesky" | custom-call | tf_op jit(solution)/shard_map/jit(cholesky)/cholesky | solution.py:8
  106.8 0.6 compare_reduce_fusion
  107.5 0.7 fusion.5
  108.1 2.4 %custom-call.7 = f32[1,32,32]{1,2,0:T(8,128)S(1)} custom-call(f32[1,32,32]{2,1,0:T(8,128)S(1)} %fusion.5), custom_call_target="InvertDiagBlocksLowerTriangular" | custom-call | tf_op jit(solution)/shard_map/jit(_solve_triangular)/triangular_solve | solution.py:9
  110.6 0.3 fusion.6
  110.9 0.0 copy-start.3
  110.9 9.6 %all-gather = f32[8,320,32]{1,2,0:T(8,128)S(1)} all-gather(f32[1,320,32]{1,2,0:T(8,128)S(1)} %bitcast.32), channel_id=1, replica_groups=mesh['dp'=4,'tensor'=8] {'tensor'}, dimensions={0}, use_global_device_ids=true | all-gather | bytes 368640 | tf_op jit(solution)/shard_map/all_gather | solution.py:21
  120.4 0.2 copy.14
  120.7 0.1 reshape.21
  120.8 11.0 %fusion = f32[1024,32]{0,1:T(8,128)} fusion(f32[2560,32]{0,1:T(8,128)S(1)} %reshape.21, f32[1,2560,1024]{2,1,0:T(8,128)} %param.4, bf16[1,2560,1024]{2,1,0:T(8,128)(2,1)} %param.3), kind=kOutput, calls=%fused_computation.1 | convolution fusion | flops 1011875840 | bytes 16187392 | tf_op jit(solution)/shard_map/dot_general | solution.py:22
  131.8 0.0 slice-start
  131.8 0.0 all-reduce.2.cloned.1.call-update
  131.8 32.1 %all-reduce.2.cloned.1.call-done = f32[1024,32]{0,1:T(8,128)} async-done(((f32[1024,32]{0,1:T(8,128)}), f32[1024,32]{0,1:T(8,128)}) %all-reduce.2.cloned.1.call-update) | async-done | bytes 131088 | tf_op jit(solution)/shard_map/psum | solution.py:23
  163.9 0.9 broadcast_multiply_fusion
  164.8 0.0 copy-start.2
  164.8 0.0 slice-start.1
  164.8 8.5 %fusion.10 = f32[2560,1024]{1,0:T(8,128)S(1)} fusion(f32[2560,32]{0,1:T(8,128)S(1)} %reshape.21, f32[1024,32]{0,1:T(8,128)S(1)} %broadcast_multiply_fusion), kind=kOutput, calls=%fused_computation.19 | convolution fusion | flops 1006632960 | bytes 10944512 | tf_op jit(solution)/shard_map/dot_general | solution.py:24
  173.3 0.0 copy-done.3
  173.4 0.0 slice-done
  173.4 0.0 slice-done.1
  173.4 0.0 copy-start.1
  173.4 12.1 %fusion.4 = f32[1,2560,1024]{2,1,0:T(8,128)} fusion(f32[2560,1024]{1,0:T(8,128)S(1)} %fusion.10, f32[1,2560,1024]{2,1,0:T(8,128)} %param.4, bf16[1,2560,1024]{2,1,0:T(8,128)(2,1)S(1)} %bitcast.31), kind=kLoop, calls=%fused_computation.5 | loop fusion | flops 7864320 | bytes 36700160 | tf_op jit(solution)/shard_map/broadcast_in_dim | solution.py:26
  185.5 0.0 copy-done.2
  185.5 0.0 copy-done.1
  (3 shorter events, 0.0 us)
Async XLA Ops:
  7.2 0.9 copy-start
  7.2 53.6 %reduce-scatter.4.cloned.1.call-start = ((), (), s32[]{:S(2)}) async-start(), calls=%async_computation.2 | async-start | bytes 1474560
  20.7 143.1 %all-reduce.2.cloned.1.call-start = ((), (), s32[]{:S(2)}) async-start(), calls=%async_computation.1 | async-start | bytes 262144 | tf_op jit(solution)/shard_map/psum | solution.py:23
  110.9 62.5 %copy-start.3 = (f32[320,32]{0,1:T(8,128)}, f32[320,32]{0,1:T(8,128)S(1)}, u32[]{:S(2)}) copy-start(f32[320,32]{0,1:T(8,128)S(1)} %fusion.6) | copy-start | bytes 122884
  131.8 41.6 %slice-start = ((s8[5242880]{0:T(1024)(128)(4,1)}), s8[1048576]{0:T(1024)(128)(4,1)S(1)}, s32[]{:S(2)}) async-start(s8[5242880]{0:T(1024)(128)(4,1)} %bitcast.30), calls=%async_computation.3 | async-start | bytes 2097152
  164.8 20.7 %copy-start.2 = (f32[1024,32]{0,1:T(8,128)}, f32[1024,32]{0,1:T(8,128)S(1)}, u32[]{:S(2)}) copy-start(f32[1024,32]{0,1:T(8,128)S(1)} %broadcast_multiply_fusion) | copy-start | bytes 393220
  164.8 8.6 %slice-start.1 = ((s8[5242880]{0:T(1024)(128)(4,1)}), s8[4194304]{0:T(1024)(128)(4,1)S(1)}, s32[]{:S(2)}) async-start(s8[5242880]{0:T(1024)(128)(4,1)} %bitcast.30), calls=%async_computation.4 | async-start | bytes 8388608
  173.4 12.1 %copy-start.1 = (f32[2560,1024]{1,0:T(8,128)}, f32[2560,1024]{1,0:T(8,128)S(1)}, u32[]{:S(2)}) copy-start(f32[2560,1024]{1,0:T(8,128)S(1)} %fusion.10) | copy-start | bytes 31457284
Sparse Core Ops, SparseCore 0:
  20.9 39.8 reduce-scatter.3
  131.9 31.8 all-reduce.1
where the time goes:
time: 193 us; the launch traced here: 192 us
  waiting for transfers between devices  72.1 us (37%)
  blocking collectives  51.4 us (27%)
  matrix products  32.6 us (17%)
  other arithmetic  19.7 us (10%)
  between operations  14.2 us (7%)
  local copies, waits for them, and re-layouts  2.32 us (1%)
    unnamed x3, waiting for transfers between devices  40 us
    psum x1, waiting for transfers between devices, local(): q_factor = lax.psum(q_local, 'dp') / lax.axis_size('dp')  32.1 us
    psum x1, blocking collectives, local(): lax.psum(jnp.dot(row_block.T, row_block, precision=high), 'tensor')  22.3 us
    psum x1, blocking collectives, local(): row_block = lax.psum(row_block, 'dp')  19.5 us
    unnamed x1, matrix products  12.6 us
    broadcast_in_dim x1, other arithmetic, local(): return (p_factor, q_factor, decoded, residual[None])  12.1 us
    dot_general x1, matrix products, local(): lax.dot_general(merged, basis_all, (((0,), (0,)), ((), ())), precision=high)  11 us
    all_gather x1, blocking collectives, local(): basis_all = lax.all_gather(p_factor, 'tensor', axis=0, tiled=True)  9.56 us
  transfers between devices with their start and end apart: 2, of which 2 were waited for; matrix products, arithmetic and copies ran while one was open for 0% of the time, Pallas kernels for 0%

commit v1 on v0

--- a/solution.py
+++ b/solution.py
@@ -20,7 +20,7 @@
     p_factor = orthonormal(row_block, gram_matrix)
     basis_all = lax.all_gather(p_factor, "tensor", axis=0, tiled=True)
     q_local = lax.dot_general(merged, basis_all, (((0,), (0,)), ((), ())), precision=high)
-    q_factor = lax.psum(q_local, "dp") / lax.axis_size("dp")
+    q_factor = jnp.sum(lax.all_gather(q_local, "dp"), axis=0) / lax.axis_size("dp")
     decoded = jnp.dot(basis_all, q_factor.T, precision=high)
     residual = merged - decoded
     return (p_factor, q_factor, decoded, residual[None])

time: 193 us -> 175 us (0.907)
  waiting for transfers between devices: 72.1 us -> 40.1 us
  blocking collectives: 51.4 us -> 67.8 us
  other arithmetic: 19.7 us -> 17.6 us
    psum x1 -> x0, waiting for transfers between devices: 32.1 us -> none  [local(): q_factor = lax.psum(q_local, 'dp') / lax.axis_size('dp')]
    all_gather x0 -> x1, blocking collectives: none -> 16.5 us  [local(): lax.all_gather(q_local, 'dp')]
    broadcast_in_dim x1, other arithmetic: 12.1 us -> 9.55 us  [local(): return (p_factor, q_factor, decoded, residual[None])]
    unnamed x3 -> x2, waiting for transfers between devices: 40 us -> 40.1 us
  transfers between devices with their start and end apart: 2 -> 1, of which waited for: 2 -> 1; matrix products, arithmetic and copies ran while one was open for 0% -> 0% of each run, Pallas kernels for 0% -> 0%
where the time goes in v1:
time: 175 us
  blocking collectives  67.8 us (39%)
  waiting for transfers between devices  40.1 us (23%)
  matrix products  31.8 us (18%)
  other arithmetic  17.6 us (10%)
  between operations  14.2 us (8%)
  local copies, waits for them, and re-layouts  3.47 us (2%)
    unnamed x2, waiting for transfers between devices  40.1 us
    psum x1, blocking collectives, local(): lax.psum(jnp.dot(row_block.T, row_block, precision=high), 'tensor')  22.3 us
    psum x1, blocking collectives, local(): row_block = lax.psum(row_block, 'dp')  19.5 us
    all_gather x1, blocking collectives, local(): lax.all_gather(q_local, 'dp')  16.5 us
    unnamed x1, matrix products  12.6 us
    dot_general x1, matrix products, local(): lax.dot_general(merged, basis_all, (((0,), (0,)), ((), ())), precision=high)  10.2 us
    all_gather x1, blocking collectives, local(): basis_all = lax.all_gather(p_factor, 'tensor', axis=0, tiled=True)  9.56 us
    broadcast_in_dim x1, other arithmetic, local(): return (p_factor, q_factor, decoded, residual[None])  9.55 us
  transfers between devices with their start and end apart: 1, of which 1 were waited for; matrix products, arithmetic and copies ran while one was open for 0% of the time, Pallas kernels for 0%

profile of v1, /device:TPU:0, one launch (start us, length us, event | category | flops | bytes accessed | tf_op | source)
XLA Modules:
  0.0 175.0 jit_solution(8001131151419898893)
XLA Ops:
  7.2 0.0 copy-start
  7.2 0.0 reduce-scatter.4.cloned.1.call-start
  7.2 0.8 copy-done
  8.1 12.6 %fusion.2 = f32[2560,32]{1,0:T(8,128)} fusion(f32[1024,32]{0,1:T(8,128)S(1)} %copy-done, f32[1,2560,1024]{2,1,0:T(8,128)} %param.4, bf16[1,2560,1024]{2,1,0:T(8,128)(2,1)} %param.3), kind=kOutput, calls=%fused_computation.3 | convolution fusion | flops 1011875840 | bytes 16187392
  20.7 0.0 reduce-scatter.4.cloned.1.call-update
  20.7 40.0 %reduce-scatter.4.cloned.1.call-done = f32[320,32]{1,0:T(8,128)} async-done(((f32[2560,32]{1,0:T(8,128)}), f32[320,32]{1,0:T(8,128)}) %reduce-scatter.4.cloned.1.call-update) | async-done | bytes 40976
  60.8 1.0 copy.17
  61.8 19.5 %psum.14 = f32[320,32]{0,1:T(8,128)S(1)} all-reduce(f32[320,32]{0,1:T(8,128)S(1)} %copy.17), channel_id=1, replica_groups=mesh['dp'=4,'tensor'=8] {'dp'}, use_global_device_ids=true, to_apply=%region_1.0 | all-reduce | flops 10240 | bytes 81920 | tf_op jit(solution)/shard_map/psum | solution.py:18
  81.3 0.2 fusion.9
  81.5 22.3 %psum.15 = f32[32,32]{0,1:T(8,128)S(1)} all-reduce(f32[32,32]{0,1:T(8,128)S(1)} %fusion.9), channel_id=1, replica_groups=mesh['dp'=4,'tensor'=8] {'tensor'}, use_global_device_ids=true, to_apply=%region_2.0 | all-reduce | flops 1024 | bytes 8192 | tf_op jit(solution)/shard_map/psum | solution.py:19
  103.8 0.1 copy.13
  103.9 2.9 %cholesky.16 = f32[32,32]{1,0:T(8,128)S(1)} custom-call(f32[32,32]{1,0:T(8,128)S(1)} %fusion.8), custom_call_target="Cholesky" | custom-call | tf_op jit(solution)/shard_map/jit(cholesky)/cholesky | solution.py:8
  106.8 0.6 compare_reduce_fusion
  107.5 0.7 fusion.5
  108.1 2.4 %custom-call.7 = f32[1,32,32]{1,2,0:T(8,128)S(1)} custom-call(f32[1,32,32]{2,1,0:T(8,128)S(1)} %fusion.5), custom_call_target="InvertDiagBlocksLowerTriangular" | custom-call | tf_op jit(solution)/shard_map/jit(_solve_triangular)/triangular_solve | solution.py:9
  110.6 0.3 fusion.6
  110.9 0.0 copy-start.3
  110.9 9.6 %all-gather.1 = f32[8,320,32]{1,2,0:T(8,128)S(1)} all-gather(f32[1,320,32]{1,2,0:T(8,128)S(1)} %bitcast.34), channel_id=1, replica_groups=mesh['dp'=4,'tensor'=8] {'tensor'}, dimensions={0}, use_global_device_ids=true | all-gather | bytes 368640 | tf_op jit(solution)/shard_map/all_gather | solution.py:21
  120.4 0.2 copy.14
  120.7 0.1 reshape.22
  120.8 10.2 %fusion = f32[1024,32]{0,1:T(8,128)S(1)} fusion(f32[2560,32]{0,1:T(8,128)S(1)} %reshape.22, f32[1,2560,1024]{2,1,0:T(8,128)} %param.4, bf16[1,2560,1024]{2,1,0:T(8,128)(2,1)} %param.3), kind=kOutput, calls=%fused_computation.1 | convolution fusion | flops 1011875840 | bytes 16187392 | tf_op jit(solution)/shard_map/dot_general | solution.py:22
  131.0 0.0 slice-start
  131.0 16.5 %all-gather = f32[4096,32]{0,1:T(8,128)S(1)} all-gather(f32[1024,32]{0,1:T(8,128)S(1)} %fusion), channel_id=2, replica_groups=mesh['dp'=4,'tensor'=8] {'dp'}, dimensions={0}, use_global_device_ids=true | all-gather | bytes 655360 | tf_op jit(solution)/shard_map/all_gather | solution.py:23
  147.4 1.1 reshape.20
  148.6 1.4 reduce_sum.9
  150.0 0.0 copy-start.2
  150.0 0.0 slice-start.1
  150.0 0.0 slice-start.2
  150.0 8.5 %fusion.10 = f32[2560,1024]{1,0:T(8,128)S(1)} fusion(f32[2560,32]{0,1:T(8,128)S(1)} %reshape.22, f32[1024,32]{0,1:T(8,128)S(1)} %broadcast_multiply_fusion), kind=kOutput, calls=%fused_computation.19 | convolution fusion | flops 1006632960 | bytes 10944512 | tf_op jit(solution)/shard_map/dot_general | solution.py:24
  158.6 0.0 copy-done.3
  158.6 0.0 slice-done
  158.6 0.0 slice-done.1
  158.6 0.0 slice-done.2
  158.6 0.0 copy-start.1
  158.6 9.5 %fusion.4 = f32[1,2560,1024]{2,1,0:T(8,128)} fusion(f32[2560,1024]{1,0:T(8,128)S(1)} %fusion.10, f32[1,2560,1024]{2,1,0:T(8,128)S(1)} %bitcast.33, bf16[1,2560,1024]{2,1,0:T(8,128)(2,1)} %param.3), kind=kLoop, calls=%fused_computation.5 | loop fusion | flops 7864320 | bytes 36700160 | tf_op jit(solution)/shard_map/broadcast_in_dim | solution.py:26
  168.2 0.0 copy-done.2
  168.2 0.0 copy-done.1
  (4 shorter events, 0.1 us)
Async XLA Ops:
  7.2 0.9 copy-start
  7.2 53.6 %reduce-scatter.4.cloned.1.call-start = ((), (), s32[]{:S(2)}) async-start(), calls=%async_computation.1 | async-start | bytes 1474560
  110.9 47.7 %copy-start.3 = (f32[320,32]{0,1:T(8,128)}, f32[320,32]{0,1:T(8,128)S(1)}, u32[]{:S(2)}) copy-start(f32[320,32]{0,1:T(8,128)S(1)} %fusion.6) | copy-start | bytes 122884
  131.0 27.6 %slice-start = ((s8[10485760]{0:T(1024)(128)(4,1)}), s8[2097152]{0:T(1024)(128)(4,1)S(1)}, s32[]{:S(2)}) async-start(s8[10485760]{0:T(1024)(128)(4,1)} %bitcast.32), calls=%async_computation.2 | async-start | bytes 4194304
  150.0 18.2 %copy-start.2 = (f32[1024,32]{0,1:T(8,128)}, f32[1024,32]{0,1:T(8,128)S(1)}, u32[]{:S(2)}) copy-start(f32[1024,32]{0,1:T(8,128)S(1)} %broadcast_multiply_fusion) | copy-start | bytes 393220
  150.0 8.6 %slice-start.1 = ((s8[10485760]{0:T(1024)(128)(4,1)}), s8[4194304]{0:T(1024)(128)(4,1)S(1)}, s32[]{:S(2)}) async-start(s8[10485760]{0:T(1024)(128)(4,1)} %bitcast.32), calls=%async_computation.3 | async-start | bytes 8388608
  150.0 8.6 %slice-start.2 = ((s8[10485760]{0:T(1024)(128)(4,1)}), s8[4194304]{0:T(1024)(128)(4,1)S(1)}, s32[]{:S(2)}) async-start(s8[10485760]{0:T(1024)(128)(4,1)} %bitcast.32), calls=%async_computation.4 | async-start | bytes 8388608
  158.6 9.6 %copy-start.1 = (f32[2560,1024]{1,0:T(8,128)}, f32[2560,1024]{1,0:T(8,128)S(1)}, u32[]{:S(2)}) copy-start(f32[2560,1024]{1,0:T(8,128)S(1)} %fusion.10) | copy-start | bytes 31457284
Sparse Core Ops, SparseCore 0:
  20.9 39.8 reduce-scatter.3
